TPU v7x, 128 devices: a whole 4x4x4 slice. The times are simulated.
128 devices in a mesh: expert: 16 (over y, x_hi, core), replica: 8 (over z, x_lo).
Axes of the slice: x: 4 (x_hi: 2, x_lo: 2; x = x_hi * 2 + x_lo), y: 4, z: 4, core: 2. Of those that a mesh axis runs over, the one named last changes fastest.
Arguments:
- tokens_in: bfloat16 [32768, 2048], P(('expert', 'replica')), may hold values from -6 to 6
- cotangents: bfloat16 [32768, 8192], P(('expert', 'replica')), may hold values from -0.1796875 to 0.1796875
- left_root: bfloat16 [16, 2048, 2048], P('expert'), may hold values from -2 to 6, as said below
- right_root: bfloat16 [16, 8, 1024, 1024], P('expert', 'replica'), may hold values from -2 to 6, as said below
Outputs:
- update: bfloat16 [16, 2048, 8192], P('expert', None, 'replica')
Inputs may be any that keep to these rules, and one draw needn't show every extreme that they name: `left_root`: each matrix is symmetric. `right_root`: each block is symmetric.
All inputs are finite; a program needn't handle non-finite values.
Results may differ from a plain program's by a relative error of at most 0.0058.
Values may be sent and summed in bfloat16 or wider, within the bound.
A program may use at most 192 MiB of HBM per device.

v0:
```python
import jax
import jax.numpy as jnp
from jax import lax
from jax.sharding import Mesh
from jax.sharding import PartitionSpec as P

REPLICA = ("replica_0", "replica_1")
EXPERT_REPLICA = ("expert", "replica_0", "replica_1")


def cut_along(value, dim, devices):
    shape = value.shape
    pieces = value.reshape(*shape[:dim], devices, shape[dim] // devices, *shape[dim + 1 :])
    return jnp.moveaxis(pieces, dim, 0)


def joined_along(pieces, dim):
    pieces = jnp.moveaxis(pieces, 0, dim)
    shape = pieces.shape
    return pieces.reshape(*shape[:dim], shape[dim] * shape[dim + 1], *shape[dim + 2 :])


def one_exchange(value, axis, axes, splits, concats):
    sizes = [lax.axis_size(a) for a in axes]
    pieces = cut_along(value, splits[0], sizes[0])
    pieces = jnp.moveaxis(cut_along(pieces, splits[1] + 1, sizes[1]), 0, 1)
    inside = pieces.shape[2:]
    pieces = pieces.reshape(-1, *inside)
    pieces = lax.all_to_all(pieces, axis, split_axis=0, concat_axis=0, tiled=True)
    pieces = joined_along(pieces.reshape(*sizes, *inside), concats[0] + 1)
    return joined_along(pieces, concats[1])


def whole_of(value, axes, dim):
    for axis in reversed(axes):
        value = lax.all_gather(value, axis, axis=dim, tiled=True)
    return value


def body(tokens_in, cotangents, left_root, right_root):
    expert_count = lax.axis_size("expert")
    replica_count = lax.axis_size(REPLICA)
    local_experts = left_root.shape[0]
    width = left_root.shape[1]
    block_count = right_root.shape[1]
    block_size = right_root.shape[2]
    columns = cotangents.shape[1] // replica_count
    slot_count = tokens_in.shape[0] // (expert_count * local_experts)
    shaped = cotangents.reshape(1, expert_count, local_experts, slot_count, replica_count, columns)
    routed = one_exchange(shaped, EXPERT_REPLICA, ("expert", REPLICA), (1, 4), (1, 0))
    routed = routed.reshape(replica_count, expert_count, local_experts, slot_count, columns)
    tokens = tokens_in.reshape(expert_count, local_experts, slot_count, width)
    grouped = lax.all_to_all(tokens, "expert", split_axis=0, concat_axis=0, tiled=True)
    gradient = jnp.einsum(
        "rnxsd,rnxsf->xdf",
        whole_of(grouped[None], REPLICA, 0),
        routed,
        preferred_element_type=jnp.float32,
    )
    gradient = gradient.astype(jnp.bfloat16)
    blocks = gradient.reshape(local_experts, width, block_count, block_size)
    applied = jnp.einsum("xdbk,xbkj->xdbj", blocks, right_root, preferred_element_type=jnp.float32)
    applied = applied.astype(jnp.bfloat16).reshape(local_experts, width, columns)
    update = jnp.einsum("xde,xef->xdf", left_root, applied, preferred_element_type=jnp.float32)
    return update.astype(jnp.bfloat16)


def solution(mesh):
    split = Mesh(
        mesh.devices.reshape(mesh.shape["expert"], 4, 2), ("expert", "replica_0", "replica_1")
    )
    placed = (
        P(EXPERT_REPLICA, None),
        P(EXPERT_REPLICA, None),
        P("expert", None, None),
        P("expert", REPLICA, None, None),
    )
    return jax.shard_map(
        body, mesh=split, in_specs=placed, out_specs=P("expert", None, REPLICA), check_vma=False
    )
```

profile of v0, /device:TPU:1, one launch (start us, length us, event | category | flops | bytes accessed | tf_op | source)
XLA Modules:
  0.0 245.0 jit_solution(10582305925600183855)
XLA Ops:
  6.5 0.0 copy-start
  6.5 0.0 all-gather.6.cloned.1.call-start
  6.5 25.4 %all_to_all.10 = bf16[16,1,16,2048]{3,2,1,0:T(8,128)(2,1)} all-to-all(bf16[16,1,16,2048]{3,2,1,0:T(8,128)(2,1)} %bitcast.54), channel_id=1, replica_groups=mesh['expert'=16,'replica_0'=4,'replica_1'=2] {'expert'}, dimensions={0} | all-to-all | bytes 2097152 | tf_op jit(solution)/shard_map/all_to_all | solution.py:53
  32.0 0.0 all-gather.6.cloned.1.call-update
  32.0 0.0 all-gather.4.cloned.1.call-start
  32.1 33.8 %all-gather.6.cloned.1.call-done = bf16[32,1,16,2048]{3,2,1,0:T(8,128)(2,1)} async-done(((bf16[16,1,16,2048]{3,2,1,0:T(8,128)(2,1)}), bf16[32,1,16,2048]{3,2,1,0:T(8,128)(2,1)}) %all-gather.6.cloned.1.call-update) | async-done | bytes 2097168 | tf_op jit(solution)/shard_map/all_gather | solution.py:36
  65.8 3.2 %copy.12 = bf16[2,16,1,16,2048]{4,3,0,1,2:T(8,128)(2,1)} copy(bf16[2,16,1,16,2048]{4,3,1,0,2:T(8,128)(2,1)} %bitcast.53) | data formatting | bytes 4194304 | tf_op jit(solution)/shard_map/all_gather | solution.py:36
  69.0 0.0 all-gather.4.cloned.1.call-update
  69.0 6.5 %copy.17 = bf16[32,8,8,1024]{3,2,1,0:T(8,128)(2,1)S(1)} copy(bf16[32,8,8,1024]{3,1,2,0:T(8,128)(2,1)} %bitcast.51) | data formatting | bytes 8388608
  75.5 2.8 %copy.13 = bf16[16,8,1,1,1,16,1,1024]{7,5,1,0,6,4,3,2:T(8,128)(2,1)S(1)} copy(bf16[16,8,1,1,1,16,1,1024]{7,1,5,0,6,4,3,2:T(8,128)(2,1)S(1)} %bitcast.50) | data formatting | bytes 8388608 | tf_op jit(solution)/shard_map/transpose;transpose | solution.py:26
  78.3 63.1 %all_to_all.11 = bf16[128,1,1,1,16,1,1024]{6,4,5,3,2,1,0:T(8,128)(2,1)} all-to-all(bf16[128,1,1,1,16,1,1024]{6,4,5,3,2,1,0:T(8,128)(2,1)S(1)} %bitcast.49), channel_id=1, replica_groups=mesh['expert'=16,'replica_0'=4,'replica_1'=2] {'expert','replica_0','rep..., dimensions={0} | all-to-all | bytes 8388608 | tf_op jit(solution)/shard_map/all_to_all | solution.py:29
  141.4 58.1 %all-gather.4.cloned.1.call-done = bf16[8,16,1,16,2048]{4,3,0,1,2:T(8,128)(2,1)} async-done(((bf16[2,16,1,16,2048]{4,3,0,1,2:T(8,128)(2,1)}), bf16[8,16,1,16,2048]{4,3,0,1,2:T(8,128)(2,1)}) %all-gather.4.cloned.1.call-update) | async-done | bytes 8388624 | tf_op jit(solution)/shard_map/all_gather | solution.py:36
  199.5 0.0 copy-done
  199.5 18.3 %fusion.4 = bf16[2048,1024]{1,0:T(8,128)(2,1)} fusion(bf16[8,16,16,1024]{3,2,0,1:T(8,128)(2,1)} %bitcast.52, bf16[8,16,1,16,2048]{4,3,0,1,2:T(8,128)(2,1)} %all-gather.4.cloned.1.call-done, bf16[1,1,1024,1024]{3,2,1,0:T(8,128)(2,1)S(1)} %copy-done), kind=kOutput, calls=%fused_computation.5 | convolution fusion | flops 12886999040 | bytes 18874368 | tf_op jit(solution)/shard_map/xdbk,xbkj->xdbj/dot_general | solution.py:62
  217.8 13.9 %convert_bitcast_fusion = bf16[1,2048,1024]{1,2,0:T(8,128)(2,1)} fusion(bf16[1,2048,2048]{2,1,0:T(8,128)(2,1)} %param.6, bf16[2048,1024]{1,0:T(8,128)(2,1)} %fusion.4), kind=kOutput, calls=%fused_computation.6 | convolution fusion | flops 8592031744 | bytes 16777216 | tf_op jit(solution)/shard_map/xde,xef->xdf/dot_general | solution.py:64
  231.7 6.4 %copy.15 = bf16[1,2048,1024]{2,1,0:T(8,128)(2,1)} copy(bf16[1,2048,1024]{1,2,0:T(8,128)(2,1)} %convert_bitcast_fusion) | data formatting | bytes 8388608 | tf_op jit(solution)/shard_map/convert_element_type | solution.py:65
Async XLA Ops:
  6.5 193.0 %copy-start = (bf16[1,1,1024,1024]{3,2,1,0:T(8,128)(2,1)S(1)}, bf16[1,1,1024,1024]{3,2,1,0:T(8,128)(2,1)}, u32[]{:S(2)}) copy-start(bf16[1,1,1024,1024]{3,2,1,0:T(8,128)(2,1)} %param.7) | copy-start | bytes 6291460
  6.5 59.3 %all-gather.6.cloned.1.call-start = ((), (), s32[]{:S(2)}) async-start(), calls=%async_computation.3 | async-start | bytes 3145728 | tf_op jit(solution)/shard_map/all_gather | solution.py:36
  32.0 167.5 %all-gather.4.cloned.1.call-start = ((), (), s32[]{:S(2)}) async-start(), calls=%async_computation.2 | async-start | bytes 10485760 | tf_op jit(solution)/shard_map/all_gather | solution.py:36
Sparse Core Ops, SparseCore 0:
  32.1 33.6 all-gather.5
  69.2 130.3 all-gather.3
where the time goes:
time: 245 us
  waiting for transfers between devices  92 us (38%)
  blocking collectives  88.5 us (36%)
  matrix products  32.2 us (13%)
  local copies, waits for them, and re-layouts  18.8 us (8%)
  between operations  13.4 us (5%)
    all_gather x2, waiting for transfers between devices, whole_of(): value = lax.all_gather(value, axis, axis=dim, tiled=True)  91.9 us
    all_to_all x1, blocking collectives, one_exchange(): lax.all_to_all(pieces, axis, split_axis=0, concat_axis=0, tiled=True)  63.1 us
    all_to_all x1, blocking collectives, body(): lax.all_to_all(tokens, 'expert', split_axis=0, concat_axis=0, tiled=True)  25.4 us
    dot_general x1, matrix products, body(): jnp.einsum('xdbk,xbkj->xdbj', blocks, right_root, preferred_element_type=...  18.3 us
    dot_general x1, matrix products, body(): jnp.einsum('xde,xef->xdf', left_root, applied, preferred_element_type=jnp...  13.9 us
    unnamed x3, local copies, waits for them, and re-layouts  6.52 us
    convert_element_type x1, local copies, waits for them, and re-layouts, body(): return update.astype(jnp.bfloat16)  6.39 us
  transfers between devices with their start and end apart: 2, of which 2 were waited for; matrix products, arithmetic and copies ran while one was open for 4% of the time, Pallas kernels for 0%

commit v1 on v0

v1 whole, which is shorter than its diff:
```python
import jax
import jax.numpy as jnp
from jax import lax
from jax.experimental import pallas as pl
from jax.experimental.pallas import tpu as pltpu
from jax.sharding import PartitionSpec as P

MESH = pl.DeviceIdType.MESH
SLOTS = 16
BOTH = ("expert", "replica")


def position():
    e, r = lax.axis_index("expert"), lax.axis_index("replica")
    return ((e // 2) % 2) * 2 + r % 2, e // 4, r // 2, e % 2


def device(x, y, z, c):
    return (y * 2 + x // 2) * 2 + c, z * 2 + x % 2


def near(x, half):
    other = (x // 2 - half) * (x // 2 - half)
    return x + other * (3 - 2 * x)


def enter(plane_sem, all_sem):
    x, y, z, c = position()
    barrier = pltpu.get_barrier_semaphore()

    def greet(k, _):
        half, up, core = k % 2, (k // 2) % 4, k // 8
        to = device(x + half * (3 - 2 * x), (y + up) % 4, z, (c + core) % 2)
        pl.semaphore_signal(barrier, inc=1, device_id=to, device_id_type=MESH)
        return 0

    lax.fori_loop(1, 16, greet, 0)
    for up in (1, 2, 3):
        pl.semaphore_signal(barrier, inc=1, device_id=device(x, y, (z + up) % 4, c), device_id_type=MESH)
    beside = x + 1 - 2 * (x % 2)
    pl.semaphore_signal(barrier, inc=1, device_id=device(beside, y, z, c), device_id_type=MESH)
    pl.semaphore_wait(barrier, 19)


def enter_all(plane_sem, all_sem):
    x, y, z, c = position()
    for up in (1, 2, 3):
        pl.semaphore_signal(plane_sem, inc=1, device_id=device(x, y, (z + up) % 4, c), device_id_type=MESH)
    pl.semaphore_wait(plane_sem, 3)
    beside = x + 1 - 2 * (x % 2)
    pl.semaphore_signal(all_sem, inc=1, device_id=device(beside, y, z, c), device_id_type=MESH)
    pl.semaphore_wait(all_sem, 1)


def exchange(tok, cot, tok_out, cot_out, send, recv, csend, crecv, plane_sem, all_sem):
    x, y, z, c = position()
    e, r = lax.axis_index("expert"), lax.axis_index("replica")
    columns = cot_out.shape[1]
    place = ((y * 2 + c) * 2 + x // 2) * SLOTS
    enter(plane_sem, all_sem)
    pltpu.make_async_copy(tok.at[pl.ds(e * SLOTS, SLOTS)], tok_out.at[pl.ds(place, SLOTS)], recv).start()

    def send_tokens(k, _):
        half, up, core = k % 2, (k // 2) % 4, k // 8
        to = device(x + half * (3 - 2 * x), (y + up) % 4, z, (c + core) % 2)
        pltpu.make_async_remote_copy(
            tok.at[pl.ds(to[0] * SLOTS, SLOTS)], tok_out.at[pl.ds(place, SLOTS)],
            send, recv, device_id=to, device_id_type=MESH,
        ).start()
        return 0

    lax.fori_loop(1, 16, send_tokens, 0)
    enter_all(plane_sem, all_sem)

    def target(half):
        return (z * 2 + near(x, half) % 2) * 16 * SLOTS + place

    pltpu.make_async_copy(
        cot.at[pl.ds(e * SLOTS, SLOTS), pl.ds(r * columns, columns)],
        cot_out.at[pl.ds(target(x // 2), SLOTS)], crecv,
    ).start()

    def send_cotangents(k, _):
        a, b, d = k % 4, (k // 4) % 4, (k // 16) % 4
        tx = (x + a) % 4
        to = device(tx, (y + a + b) % 4, (z + a + d) % 4, (c + k // 64) % 2)
        pltpu.make_async_remote_copy(
            cot.at[pl.ds(to[0] * SLOTS, SLOTS), pl.ds(to[1] * columns, columns)],
            cot_out.at[pl.ds(target(tx // 2), SLOTS)],
            csend, crecv, device_id=to, device_id_type=MESH,
        ).start()
        return 0

    lax.fori_loop(1, 128, send_cotangents, 0)
    pltpu.make_async_copy(tok_out, tok_out, recv).wait()
    most = tok_out.at[pl.ds(0, 15 * SLOTS)]
    pltpu.make_async_copy(most, most, send).wait()
    pltpu.make_async_copy(cot_out, cot_out, crecv).wait()
    most = cot_out.at[pl.ds(0, 127 * SLOTS)]
    pltpu.make_async_copy(most, most, csend).wait()


def body(tokens_in, cotangents, left_root, right_root):
    rows, width = tokens_in.shape
    columns = cotangents.shape[1] // lax.axis_size("replica")
    tokens, routed = pl.pallas_call(
        exchange,
        out_shape=(
            jax.ShapeDtypeStruct((rows, width), jnp.bfloat16),
            jax.ShapeDtypeStruct((rows * 8, columns), jnp.bfloat16),
        ),
        in_specs=[pl.BlockSpec(memory_space=pl.ANY)] * 2,
        out_specs=[pl.BlockSpec(memory_space=pltpu.VMEM)] * 2,
        scratch_shapes=[pltpu.SemaphoreType.DMA] * 4 + [pltpu.SemaphoreType.REGULAR] * 2,
        compiler_params=pltpu.CompilerParams(collective_id=0, has_side_effects=True),
    )(tokens_in, cotangents)
    left = lax.dot_general(
        left_root[0], tokens, (((1,), (1,)), ((), ())), preferred_element_type=jnp.float32
    ).astype(jnp.bfloat16)
    gathered = lax.all_gather(left, "replica", axis=0, tiled=False)
    right = jnp.dot(routed, right_root[0, 0], preferred_element_type=jnp.float32).astype(jnp.bfloat16)
    right = right.reshape(8, rows, columns)
    update = jnp.einsum("qdt,qtf->df", gathered, right, preferred_element_type=jnp.float32)
    return update.astype(jnp.bfloat16)[None]


def solution(mesh):
    placed = (
        P(BOTH, None),
        P(BOTH, None),
        P("expert", None, None),
        P("expert", "replica", None, None),
    )
    return jax.shard_map(
        body, mesh=mesh, in_specs=placed, out_specs=P("expert", None, "replica"), check_vma=False
    )
```

time: 245 us -> 301 us (1.23)
  blocking collectives: 88.5 us -> 0 us
  Pallas kernels: 0 us -> 75.1 us
  waiting for transfers between devices: 92 us -> 157 us
  local copies, waits for them, and re-layouts: 18.8 us -> 24.5 us
    all_to_all x2 -> x0, blocking collectives: 88.5 us -> none  [the longest x1 63.1 us: one_exchange(): lax.all_to_all(pieces, axis, split_axis=0, concat_axis=0, tiled=True)]
    pallas_call x0 -> x1, Pallas kernels: none -> 75.1 us  [body(): pl.pallas_call(exchange, out_shape=(jax.ShapeDtypeStruct((rows, width), j...]
    all_gather x2 -> x1, waiting for transfers between devices: 91.9 us -> 157 us  [body(): gathered = lax.all_gather(left, 'replica', axis=0, tiled=False)]
    all_gather x1 -> x2, local copies, waits for them, and re-layouts: 3.16 us -> 24.4 us  [body(): gathered = lax.all_gather(left, 'replica', axis=0, tiled=False)]
    unnamed x3 -> x2, local copies, waits for them, and re-layouts: 6.52 us -> 0.01 us
    convert_element_type x1 -> x0, local copies, waits for them, and re-layouts: 6.39 us -> none  [body(): return update.astype(jnp.bfloat16)]
    dot_general x2 -> x3, matrix products: 32.2 us -> 30.1 us  [the longest x1 14.7 us: body(): jnp.einsum('qdt,qtf->df', gathered, right, preferred_element_type=jnp.flo...]
  transfers between devices with their start and end apart: 2 -> 1, of which waited for: 2 -> 1; matrix products, arithmetic and copies ran while one was open for 4% -> 3% of each run, Pallas kernels for 0% -> 0%
where the time goes in v1:
time: 301 us; the launch traced here: 300 us
  waiting for transfers between devices  157 us (52%)
  Pallas kernels  75.1 us (25%)
  matrix products  30.1 us (10%)
  local copies, waits for them, and re-layouts  24.5 us (8%)
  between operations  13.4 us (4%)
    all_gather x1, waiting for transfers between devices, body(): gathered = lax.all_gather(left, 'replica', axis=0, tiled=False)  157 us
    pallas_call x1, Pallas kernels, body(): pl.pallas_call(exchange, out_shape=(jax.ShapeDtypeStruct((rows, width), j...  75.1 us
    all_gather x2, local copies, waits for them, and re-layouts, body(): gathered = lax.all_gather(left, 'replica', axis=0, tiled=False)  24.4 us
    dot_general x1, matrix products, body(): jnp.einsum('qdt,qtf->df', gathered, right, preferred_element_type=jnp.flo...  14.7 us
    dot_general x1, matrix products, body(): jnp.dot(routed, right_root[0, 0], preferred_element_type=jnp.float32)  8.32 us
    dot_general x1, matrix products, body(): lax.dot_general(left_root[0], tokens, (((1,), (1,)), ((), ())), preferred...  7.05 us
  transfers between devices with their start and end apart: 1, of which 1 were waited for; matrix products, arithmetic and copies ran while one was open for 3% of the time, Pallas kernels for 0%

profile of v1, /device:TPU:1, one launch (start us, length us, event | category | flops | bytes accessed | tf_op | source)
XLA Modules:
  0.0 300.4 jit_solution(258526028124671044)
XLA Ops:
  6.5 0.0 copy-start
  6.5 0.0 all-gather.3.cloned.1.call-start
  6.5 75.1 %shard_map.46 = (bf16[256,2048]{1,0:T(8,128)(2,1)}, bf16[2048,1024]{1,0:T(8,128)(2,1)}) custom-call(bf16[256,2048]{1,0:T(8,128)(2,1)} %tok.1, bf16[256,8192]{1,0:T(8,128)(2,1)} %cot.1), custom_call_target="tpu_custom_call" | custom-call | tf_op jit(solution)/shard_map/pallas_call | solution.py:106
  81.6 7.1 %fusion.9 = bf16[2048,256]{0,1:T(8,128)(2,1)} fusion(bf16[256,2048]{1,0:T(8,128)(2,1)} %get-tuple-element.7, bf16[1,2048,2048]{2,1,0:T(8,128)(2,1)} %param.6), kind=kOutput, calls=%fused_computation.7 | convolution fusion | flops 2148007936 | bytes 10485760 | tf_op jit(solution)/shard_map/dot_general | solution.py:117
  88.7 0.0 all-gather.3.cloned.1.call-update
  88.7 0.0 copy-done
  88.7 8.3 %convolution_convert_fusion = bf16[2048,1024]{1,0:T(8,128)(2,1)} fusion(bf16[2048,1024]{1,0:T(8,128)(2,1)} %get-tuple-element.8, bf16[1,1,1024,1024]{3,2,1,0:T(8,128)(2,1)S(1)} %copy-done), kind=kOutput, calls=%fused_computation.4 | convolution fusion | flops 4297064448 | bytes 10485760 | tf_op jit(solution)/shard_map/dot_general | solution.py:121
  97.0 157.4 %all-gather.3.cloned.1.call-done = bf16[16384,256]{0,1:T(8,128)(2,1)} async-done(((bf16[2048,256]{0,1:T(8,128)(2,1)}), bf16[16384,256]{0,1:T(8,128)(2,1)}) %all-gather.3.cloned.1.call-update) | async-done | bytes 8388624 | tf_op jit(solution)/shard_map/all_gather | solution.py:120
  254.4 11.9 %copy.8 = bf16[16384,256]{1,0:T(8,128)(2,1)} copy(bf16[16384,256]{0,1:T(8,128)(2,1)} %all-gather.3.cloned.1.call-done) | data formatting | bytes 16777216 | tf_op jit(solution)/shard_map/all_gather | solution.py:120
  266.3 12.5 %copy.6 = bf16[8,2048,256]{1,0,2:T(8,128)(2,1)} copy(bf16[8,2048,256]{2,1,0:T(8,128)(2,1)} %bitcast.23) | data formatting | bytes 16777216 | tf_op jit(solution)/shard_map/all_gather | solution.py:120
  278.8 14.7 %fusion.3 = bf16[1,2048,1024]{2,1,0:T(8,128)(2,1)} fusion(bf16[8,2048,256]{1,0,2:T(8,128)(2,1)} %copy.6, bf16[8,256,1024]{2,1,0:T(8,128)(2,1)} %bitcast.24), kind=kOutput, calls=%fused_computation.5 | convolution fusion | flops 8592031744 | bytes 16777216 | tf_op jit(solution)/shard_map/qdt,qtf->df/dot_general | solution.py:123
Async XLA Ops:
  6.5 82.2 %copy-start = (bf16[1,1,1024,1024]{3,2,1,0:T(8,128)(2,1)S(1)}, bf16[1,1,1024,1024]{3,2,1,0:T(8,128)(2,1)}, u32[]{:S(2)}) copy-start(bf16[1,1,1024,1024]{3,2,1,0:T(8,128)(2,1)} %param.7) | copy-start | bytes 6291460
  6.5 247.8 %all-gather.3.cloned.1.call-start = ((), (), s32[]{:S(2)}) async-start(), calls=%async_computation | async-start | bytes 9437184 | tf_op jit(solution)/shard_map/all_gather | solution.py:120
Sparse Core Ops, SparseCore 0:
  88.8 165.5 all-gather.2

commit v2 on v1

v2 whole, which is shorter than its diff:
```python
import functools

import jax
import jax.numpy as jnp
from jax import lax
from jax.experimental import pallas as pl
from jax.experimental.pallas import tpu as pltpu
from jax.sharding import PartitionSpec as P

MESH = pl.DeviceIdType.MESH
SLOTS = 16
BOTH = ("expert", "replica")
TILE = 256
FIRST = 1152
STEPS = ((2, 0), (2, 1), (1, 0), (1, 1), (3, 0), (3, 1), (0, 0), (0, 1))
EARLY = 3


def position():
    e, r = lax.axis_index("expert"), lax.axis_index("replica")
    return ((e // 2) % 2) * 2 + r % 2, e // 4, r // 2, e % 2


def device(x, y, z, c):
    return (y * 2 + x // 2) * 2 + c, z * 2 + x % 2


def near(x, half):
    other = (x // 2 - half) * (x // 2 - half)
    return x + other * (3 - 2 * x)


def signal(semaphore, to):
    pl.semaphore_signal(semaphore, inc=1, device_id=to, device_id_type=MESH)


def drain(ref, semaphore):
    pltpu.make_async_copy(ref, ref, semaphore).wait()


def kernel(
    tok, cot, left_hbm, right_hbm, out,
    left, right, tokens, routed, lefts, rights, total,
    load, tok_send, tok_recv, cot_send, cot_recv, send, recv, plane_sem, all_sem,
):
    x, y, z, c = position()
    e, r = lax.axis_index("expert"), lax.axis_index("replica")
    columns = rights.shape[2]
    rows = tokens.shape[0]
    depth = left.shape[0]
    place = ((y * 2 + c) * 2 + x // 2) * SLOTS
    beside = x + 1 - 2 * (x % 2)
    bx = beside % 2
    mx = x % 2
    above, below = (z + 1) % 4, (z + 3) % 4

    load_left = pltpu.make_async_copy(left_hbm, left, load.at[0])
    load_right = pltpu.make_async_copy(right_hbm, right, load.at[1])
    load_left.start()
    load_right.start()

    barrier = pltpu.get_barrier_semaphore()

    def token_peer(k):
        half, up, core = k % 2, (k // 2) % 4, k // 8
        return device(x + half * (3 - 2 * x), (y + up) % 4, z, (c + core) % 2)

    def greet(k, _):
        signal(barrier, token_peer(k))
        return 0

    lax.fori_loop(1, 16, greet, 0)
    for up in (1, 2, 3):
        signal(barrier, device(x, y, (z + up) % 4, c))
    signal(barrier, device(beside, y, z, c))
    pl.semaphore_wait(barrier, 19)
    for up in (1, 2, 3):
        signal(plane_sem, device(x, y, (z + up) % 4, c))

    def send_tokens(k, _):
        to = token_peer(k)
        pltpu.make_async_remote_copy(
            tok.at[pl.ds(to[0] * SLOTS, SLOTS)], tokens.at[pl.ds(place, SLOTS)],
            tok_send, tok_recv, device_id=to, device_id_type=MESH,
        ).start()
        return 0

    lax.fori_loop(1, 16, send_tokens, 0)
    pltpu.make_async_copy(tok.at[pl.ds(e * SLOTS, SLOTS)], tokens.at[pl.ds(place, SLOTS)], tok_recv).start()
    pl.semaphore_wait(plane_sem, 3)
    signal(all_sem, device(beside, y, z, c))
    pl.semaphore_wait(all_sem, 1)

    def chunk_of(half):
        return z * 2 + near(x, half) % 2

    pltpu.make_async_copy(
        cot.at[pl.ds(e * SLOTS, SLOTS), pl.ds(r * columns, columns)],
        routed.at[chunk_of(x // 2), pl.ds(place, SLOTS)], cot_recv.at[chunk_of(x // 2)],
    ).start()

    def send_cotangents(step):
        lift, core = STEPS[step]

        def one(k, _):
            a, b = k % 4, k // 4
            tx = (x + a) % 4
            to = device(tx, (y + a + b) % 4, (z + a + lift) % 4, (c + core) % 2)
            chunk = chunk_of(tx // 2)
            pltpu.make_async_remote_copy(
                cot.at[pl.ds(to[0] * SLOTS, SLOTS), pl.ds(to[1] * columns, columns)],
                routed.at[chunk, pl.ds(place, SLOTS)],
                cot_send.at[step], cot_recv.at[chunk], device_id=to, device_id_type=MESH,
            ).start()
            return 0

        lax.fori_loop(1 if STEPS[step] == (0, 0) else 0, 16, one, 0)

    def sent_cotangents(step):
        size = 15 if STEPS[step] == (0, 0) else 16
        drain(routed.at[0, pl.ds(0, size * SLOTS)], cot_send.at[step])

    parts = {"a": (0, FIRST), "b": (FIRST, depth - FIRST)}
    half = (depth - FIRST) // 2
    if half:
        parts["c"] = (FIRST, half)
        parts["d"] = (FIRST + half, half)
    names = [(s, dz, p) for s in (0, 1) for dz in (0, 1, 2, 3) for p in "abcd"]
    flight = []

    def block(s, dz, part):
        start, size = parts[part]
        return lefts.at[((z + dz) % 4) * 2 + (bx if s else mx), pl.ds(start, size)]

    def push(s, dz, part, to):
        if parts[part][1] == 0:
            return
        if to == "beside":
            there, name = device(beside, y, z, c), (1 - s, dz, part)
        elif to == "above":
            there, name = device(x, y, above, c), (s, (dz + 3) % 4, part)
        else:
            there, name = device(x, y, below, c), (s, (dz + 1) % 4, part)
        ref = block(s, dz, part)
        copy = pltpu.make_async_remote_copy(
            ref, ref, send.at[len(flight)], recv.at[names.index(name)],
            device_id=there, device_id_type=MESH,
        )
        copy.start()
        flight.append((ref, send.at[len(flight)]))

    def arrived(s, dz, part):
        if parts[part][1]:
            drain(block(s, dz, part), recv.at[names.index((s, dz, part))])

    def apply_left(start, size):
        @pl.loop(0, size, step=TILE // 2)
        def _(row):
            at = pl.ds(start + row, TILE // 2)
            lefts[r, at] = lax.dot_general(
                left[at], tokens[...], (((1,), (1,)), ((), ())), preferred_element_type=jnp.float32
            ).astype(jnp.bfloat16)

    def apply_right(chunk):
        drain(routed.at[chunk], cot_recv.at[chunk])
        rights[chunk] = jnp.dot(
            routed[chunk], right[...], preferred_element_type=jnp.float32
        ).astype(jnp.bfloat16)

    def accumulate(chunks, part, first=False, last=False):
        start, size = parts[part]

        @pl.loop(0, size, step=TILE // 2)
        def _(row):
            at = pl.ds(start + row, TILE // 2)
            value = None if first else total[at]
            for chunk in chunks:
                term = jnp.dot(lefts[chunk, at], rights[chunk], preferred_element_type=jnp.float32)
                value = term if value is None else value + term
            if last:
                out[at] = value.astype(out.dtype)
            else:
                total[at] = value

    def chunk(s, dz):
        return ((z + dz) % 4) * 2 + (bx if s else mx)

    for step in range(EARLY):
        send_cotangents(step)
    drain(tokens, tok_recv)
    load_left.wait()
    apply_left(*parts["a"])
    if half:
        apply_left(*parts["b"])
    push(0, 0, "a", "beside")
    push(0, 0, "b", "above")
    push(0, 0, "b", "below")
    push(0, 0, "a", "above")
    push(0, 0, "a", "below")
    push(0, 0, "b", "beside")
    for step in range(EARLY, 8):
        sent_cotangents(step - EARLY)
        send_cotangents(step)
        if step == EARLY + 1:
            arrived(1, 0, "a")
            push(1, 0, "a", "above")
            push(1, 0, "a", "below")
    if half:
        arrived(0, 3, "b")
        push(0, 3, "c", "above")
        push(0, 3, "b", "beside")
        arrived(0, 1, "b")
        push(0, 1, "d", "below")
        push(0, 1, "b", "beside")
    arrived(0, 3, "a")
    push(0, 3, "a", "above")
    arrived(1, 1, "a")
    push(1, 1, "a", "below")
    if half:
        arrived(0, 2, "c")
        push(0, 2, "c", "beside")
        arrived(0, 2, "d")
        push(0, 2, "d", "beside")
    load_right.wait()
    for s in (0, 1):
        for dz in (0, 1, 3, 2):
            apply_right(chunk(s, dz))
    both = lambda dz: [chunk(0, dz), chunk(1, dz)]
    if half:
        arrived(1, 0, "b")
    accumulate(both(0), "a", first=True)
    accumulate(both(0), "b", first=True)
    arrived(1, 3, "a")
    arrived(0, 1, "a")
    if half:
        arrived(1, 1, "b")
        arrived(1, 3, "b")
    for part in "ab":
        accumulate(both(1) + both(3), part)
    arrived(0, 2, "a")
    arrived(1, 2, "a")
    accumulate(both(2), "a", last=True)
    if half:
        arrived(1, 2, "c")
        arrived(1, 2, "d")
        accumulate(both(2), "b", last=True)

    drain(tokens.at[pl.ds(0, 15 * SLOTS)], tok_send)
    for step in range(8 - EARLY, 8):
        sent_cotangents(step)
    for ref, semaphore in flight:
        drain(ref, semaphore)


def body(tokens_in, cotangents, left_root, right_root):
    rows, depth = tokens_in.shape
    columns = right_root.shape[3]
    bf16 = jnp.bfloat16
    update = pl.pallas_call(
        kernel,
        out_shape=jax.ShapeDtypeStruct((depth, columns), bf16),
        in_specs=[pl.BlockSpec(memory_space=pl.ANY)] * 4,
        out_specs=pl.BlockSpec(memory_space=pltpu.VMEM),
        scratch_shapes=[
            pltpu.VMEM((depth, depth), bf16),
            pltpu.VMEM((columns, columns), bf16),
            pltpu.VMEM((rows, depth), bf16),
            pltpu.VMEM((8, rows, columns), bf16),
            pltpu.VMEM((8, depth, rows), bf16),
            pltpu.VMEM((8, rows, columns), bf16),
            pltpu.VMEM((depth, columns), jnp.float32),
            pltpu.SemaphoreType.DMA((2,)),
            pltpu.SemaphoreType.DMA,
            pltpu.SemaphoreType.DMA,
            pltpu.SemaphoreType.DMA((8,)),
            pltpu.SemaphoreType.DMA((8,)),
            pltpu.SemaphoreType.DMA((24,)),
            pltpu.SemaphoreType.DMA((32,)),
            pltpu.SemaphoreType.REGULAR,
            pltpu.SemaphoreType.REGULAR,
        ],
        compiler_params=pltpu.CompilerParams(
            collective_id=0, has_side_effects=True, vmem_limit_bytes=60 << 20
        ),
    )(tokens_in, cotangents, left_root[0], right_root[0, 0])
    return update[None]


def solution(mesh):
    placed = (
        P(BOTH, None),
        P(BOTH, None),
        P("expert", None, None),
        P("expert", "replica", None, None),
    )
    return jax.shard_map(
        body, mesh=mesh, in_specs=placed, out_specs=P("expert", None, "replica"), check_vma=False
    )
```

time: 301 us -> 143 us (0.48)
  waiting for transfers between devices: 157 us -> 0 us
  Pallas kernels: 75.1 us -> 138 us
  matrix products: 30.1 us -> 0 us
  local copies, waits for them, and re-layouts: 24.5 us -> 4.64 us
  between operations: 13.4 us -> 0.01 us
    all_gather x1 -> x0, waiting for transfers between devices: 157 us -> none  [body(): gathered = lax.all_gather(left, 'replica', axis=0, tiled=False)]
    pallas_call x1, Pallas kernels: 75.1 us -> 138 us  [body(): pl.pallas_call(kernel, out_shape=jax.ShapeDtypeStruct((depth, columns), b...]
    dot_general x3 -> x0, matrix products: 30.1 us -> none  [the longest x1 14.7 us: body(): jnp.einsum('qdt,qtf->df', gathered, right, preferred_element_type=jnp.flo...]
    all_gather x2 -> x0, local copies, waits for them, and re-layouts: 24.4 us -> none  [body(): gathered = lax.all_gather(left, 'replica', axis=0, tiled=False)]
    unnamed x2 -> x1, local copies, waits for them, and re-layouts: 0.01 us -> 4.64 us
  transfers between devices with their start and end apart: 1 -> 0, of which waited for: 1 -> 0; matrix products, arithmetic and copies ran while one was open for 3% -> 0% of each run, Pallas kernels for 0% -> 0%
where the time goes in v2:
time: 143 us
  Pallas kernels  138 us (97%)
  local copies, waits for them, and re-layouts  4.64 us (3%)
    pallas_call x1, Pallas kernels, body(): pl.pallas_call(kernel, out_shape=jax.ShapeDtypeStruct((depth, columns), b...  138 us
    unnamed x1, local copies, waits for them, and re-layouts  4.64 us

profile of v2, /device:TPU:1, one launch (start us, length us, event | category | flops | bytes accessed | tf_op | source)
XLA Modules:
  0.0 142.6 jit_solution(9290802780222366541)
XLA Ops:
  0.0 137.9 %shard_map.46 = bf16[2048,1024]{1,0:T(8,128)(2,1)} custom-call(bf16[256,2048]{1,0:T(8,128)(2,1)} %tok.1, bf16[256,8192]{1,0:T(8,128)(2,1)} %cot.1, bf16[2048,2048]{1,0:T(8,128)(2,1)} %bitcast.4, bf16[1024,1024]{1,0:T(8,128)(2,1)} %bitcast.5), custom_call_target="tpu_custom_call" | custom-call | tf_op jit(solution)/shard_map/pallas_call | solution.py:259
  137.9 4.6 %copy.6 = bf16[1,2048,1024]{2,1,0:T(8,128)(2,1)} copy(bf16[1,2048,1024]{2,1,0:T(8,128)(2,1)} %bitcast.3) | data formatting | bytes 8388608

commit v3 on v1

v3 whole, which is shorter than its diff:
```python
import functools

import jax
import jax.numpy as jnp
from jax import lax
from jax.experimental import pallas as pl
from jax.experimental.pallas import tpu as pltpu
from jax.sharding import PartitionSpec as P

MESH = pl.DeviceIdType.MESH
SLOTS = 16
BOTH = ("expert", "replica")
GROUPS = ((352, 272), (320, 256), (272, 208), (208, 160))
PIECES = len(GROUPS)
ROUTED = ()
OWN = ((0, 1), (2,), (3,), (), (), (), ())
STEPS = ((2, 0), (2, 1), (1, 0), (1, 1), (3, 0), (3, 1), (0, 0), (0, 1))
PLAN = ((1, 2, 3, 4), (5, 6, 7), (), (), (), (), ())
LAG = 6
RIGHTS = (0, 0, 0, 4, 0, 0, 0)
FINISH = ((), (), (), (0,), (1,), (2,), ())


def pieces():
    spans, start = {}, 0
    for i, (first, second) in enumerate(GROUPS):
        spans["a", i] = (start, first)
        spans["b", i] = (start + first, second)
        spans[i] = (start, first + second)
        start += first + second
    return spans


def product(lefts, rights, at, out):
    @pl.loop(0, rights.shape[2], step=256)
    def _(column):
        to = pl.ds(pl.multiple_of(column, 256), 256)
        value = None
        for q in range(8):
            term = jnp.dot(lefts[q, at], rights[q, :, to], preferred_element_type=jnp.float32)
            value = term if value is None else value + term
        out[:, to] = value.astype(out.dtype)


def position():
    e, r = lax.axis_index("expert"), lax.axis_index("replica")
    return ((e // 2) % 2) * 2 + r % 2, e // 4, r // 2, e % 2


def device(x, y, z, c):
    return (y * 2 + x // 2) * 2 + c, z * 2 + x % 2


def near(x, half):
    other = (x // 2 - half) * (x // 2 - half)
    return x + other * (3 - 2 * x)


def signal(semaphore, to):
    pl.semaphore_signal(semaphore, inc=1, device_id=to, device_id_type=MESH)


def drain(ref, semaphore):
    pltpu.make_async_copy(ref, ref, semaphore).wait()


def kernel(
    tok, cot, left_hbm, right_hbm, out, lefts, rights,
    left, right, tokens, routed,
    load, tok_send, tok_recv, cot_send, cot_recv, send, recv, plane_sem, all_sem,
):
    x, y, z, c = position()
    e, r = lax.axis_index("expert"), lax.axis_index("replica")
    columns = rights.shape[2]
    depth = left.shape[0]
    place = ((y * 2 + c) * 2 + x // 2) * SLOTS
    beside = x + 1 - 2 * (x % 2)

    load_left = pltpu.make_async_copy(left_hbm, left, load.at[0])
    load_right = pltpu.make_async_copy(right_hbm, right, load.at[1])
    load_left.start()
    load_right.start()

    barrier = pltpu.get_barrier_semaphore()

    def token_peer(k):
        half, up, core = k % 2, (k // 2) % 4, k // 8
        return device(x + half * (3 - 2 * x), (y + up) % 4, z, (c + core) % 2)

    def greet(k, _):
        signal(barrier, token_peer(k))
        return 0

    lax.fori_loop(1, 16, greet, 0)
    for up in (1, 2, 3):
        signal(barrier, device(x, y, (z + up) % 4, c))
    signal(barrier, device(beside, y, z, c))
    pl.semaphore_wait(barrier, 19)
    for up in (1, 2, 3):
        signal(plane_sem, device(x, y, (z + up) % 4, c))

    def send_tokens(k, _):
        to = token_peer(k)
        pltpu.make_async_remote_copy(
            tok.at[pl.ds(to[0] * SLOTS, SLOTS)], tokens.at[pl.ds(place, SLOTS)],
            tok_send, tok_recv, device_id=to, device_id_type=MESH,
        ).start()
        return 0

    lax.fori_loop(1, 16, send_tokens, 0)
    pltpu.make_async_copy(tok.at[pl.ds(e * SLOTS, SLOTS)], tokens.at[pl.ds(place, SLOTS)], tok_recv).start()
    pl.semaphore_wait(plane_sem, 3)
    signal(all_sem, device(beside, y, z, c))
    pl.semaphore_wait(all_sem, 1)

    def chunk_of(half):
        return z * 2 + near(x, half) % 2

    pltpu.make_async_copy(
        cot.at[pl.ds(e * SLOTS, SLOTS), pl.ds(r * columns, columns)],
        routed.at[chunk_of(x // 2), pl.ds(place, SLOTS)], cot_recv.at[chunk_of(x // 2)],
    ).start()

    def send_one(step, turn, up, lift, core):
        over = turn // 2
        side = ((turn + 1) // 2) % 2
        high, low = x // 2 + over - 2 * over * (x // 2), x % 2 + side - 2 * side * (x % 2)
        to = device(high * 2 + low, (y + up) % 4, (z + lift) % 4, (c + core) % 2)
        chunk = chunk_of(high)
        pltpu.make_async_remote_copy(
            cot.at[pl.ds(to[0] * SLOTS, SLOTS), pl.ds(to[1] * columns, columns)],
            routed.at[chunk, pl.ds(place, SLOTS)],
            cot_send.at[step], cot_recv.at[chunk], device_id=to, device_id_type=MESH,
        ).start()

    def send_near():
        def one(k, _):
            send_one(8, k % 2, 0, (k // 2) % 4, k // 8)
            return 0

        lax.fori_loop(1, 16, one, 0)

    def send_far(step):
        lift, core = STEPS[step]

        def one(k, _):
            a, b = k % 4, k // 4
            send_one(step, a, (a + b) % 4, (a + lift) % 4, core)
            return 0

        lax.fori_loop(1, 13, one, 0)
        lax.fori_loop(14, 16, one, 0)

    def sent(step):
        drain(routed.at[0, pl.ds(0, (15 if step == 8 else 14) * SLOTS)], cot_send.at[step])

    parts = pieces()
    names = [(s, dz, (p, i)) for s in (0, 1) for dz in (0, 1, 2, 3) for p in "ab" for i in range(PIECES)]
    flight = {}

    def chunk(s, dz):
        return ((z + dz) % 4) * 2 + (beside if s else x) % 2

    def block(s, dz, part):
        return lefts.at[chunk(s, dz), pl.ds(*parts[part])]

    def push(s, dz, part, to):
        if to == "beside":
            there, name = device(beside, y, z, c), (1 - s, dz, part)
        elif to == "above":
            there, name = device(x, y, (z + 1) % 4, c), (s, (dz + 3) % 4, part)
        elif to == "below":
            there, name = device(x, y, (z + 3) % 4, c), (s, (dz + 1) % 4, part)
        else:
            there, name = device(x, y, (z + 2) % 4, c), (s, (dz + 2) % 4, part)
        ref = block(s, dz, part)
        kind = (s, dz > 0, part[0] == "a", to == "beside")
        rows = flight.setdefault(kind, [])
        rows.append(parts[part][1])
        pltpu.make_async_remote_copy(
            ref, ref, send.at[list(flight).index(kind)], recv.at[names.index(name)],
            device_id=there, device_id_type=MESH,
        ).start()

    def arrived(s, dz, part):
        drain(block(s, dz, part), recv.at[names.index((s, dz, part))])

    def apply_left(part):
        at = pl.ds(*parts[part])
        lefts[r, at] = lax.dot_general(
            left[at], tokens[...], (((1,), (1,)), ((), ())), preferred_element_type=jnp.float32
        ).astype(jnp.bfloat16)

    def apply_right(dz):
        at = pl.ds(((z + dz) % 4) * 2, 2)
        for s in (0, 1):
            drain(routed.at[chunk(s, dz)], cot_recv.at[chunk(s, dz)])
        both = routed[at].reshape(512, columns)
        rights[at] = jnp.dot(both, right[...], preferred_element_type=jnp.float32).astype(
            jnp.bfloat16
        ).reshape(2, 256, columns)

    def multiply(part):
        at = pl.ds(*parts[part])
        product(lefts, rights, at, out.at[at])

    def push_own(part):
        for to in ("beside", "above", "below") if part[0] == "a" else ("above", "below", "beside"):
            push(0, 0, part, to)
        if part[1] in ROUTED:
            push(0, 0, part, "over")

    waited = []

    def far(steps):
        for step in steps:
            old = 8 if step == LAG - 1 else step - LAG
            if old >= 0:
                sent(old)
                waited.append(old)
            send_far(step)

    turns = [0, 1, 3, 2]

    def some_right(count):
        for _ in range(count):
            if len(turns) == 4:
                load_right.wait()
            apply_right(turns.pop(0))

    def arrivals(i):
        part = ("a", i)
        late = ((0, 3), (1, 1)) if i in ROUTED else ()
        for s, dz in late + ((1, 3), (0, 1), (0, 2), (1, 2)):
            arrived(s, dz, part)
        part = ("b", i)
        for dz in (0, 1, 3, 2):
            arrived(1, dz, part)

    def push_group(i):
        push_own(("a", i))
        push_own(("b", i))

    ready = [0]

    def prepare(upto):
        while ready[0] < min(upto, PIECES):
            apply_left(ready[0])
            ready[0] += 1

    send_near()
    drain(tokens.at[pl.ds(0, 15 * SLOTS)], tok_send)
    send_far(0)
    load_left.wait()
    drain(tokens, tok_recv)
    prepare(1)
    for step in range(PIECES + 3):
        last, older = (i if 0 <= i < PIECES else None for i in (step - 1, step - 2))
        if older is not None and older not in ROUTED:
            arrived(0, 3, ("a", older))
            push(0, 3, ("a", older), "above")
            arrived(1, 1, ("a", older))
            push(1, 1, ("a", older), "below")
        if last is not None:
            part = ("a", last)
            arrived(1, 0, part)
            push(1, 0, part, "above")
            push(1, 0, part, "below")
            if last in ROUTED:
                push(1, 0, part, "over")
            part = ("b", last)
            arrived(0, 3, part)
            arrived(0, 1, part)
            if last not in ROUTED:
                if last % 2:
                    push(0, 1, part, "below")
                else:
                    push(0, 3, part, "above")
            push(0, 1, part, "beside")
            push(0, 3, part, "beside")
            if last in ROUTED:
                arrived(0, 2, part)
                push(0, 2, part, "beside")
        for own in OWN[step]:
            prepare(own + 2)
            push_group(own)
        far(PLAN[step])
        if older is not None and older not in ROUTED:
            part = ("b", older)
            arrived(0, 2, part)
            push(0, 2, part, "beside")
        some_right(RIGHTS[step])
        for i in FINISH[step]:
            arrivals(i)
            multiply(i)
    arrivals(PIECES - 1)

    for step in range(9):
        if step not in waited:
            sent(step)
    for i, rows in enumerate(flight.values()):
        times = next(n for n in (1, 2, 3, 4, 5, 6, 7, 8) if sum(rows) % n == 0 and sum(rows) // n <= depth)
        drain(lefts.at[pl.ds(0, times), pl.ds(0, sum(rows) // times)], send.at[i])


def ending(done, lefts, rights, out, rest, sems):
    start, size = pieces()[PIECES - 1]
    whole = pltpu.make_async_copy(done.at[pl.ds(0, start)], out.at[pl.ds(0, start)], sems.at[0])
    whole.start()
    product(lefts, rights, pl.ds(start, size), rest)
    last = pltpu.make_async_copy(rest, out.at[pl.ds(start, size)], sems.at[1])
    last.start()
    whole.wait()
    last.wait()


def body(tokens_in, cotangents, left_root, right_root):
    rows, depth = tokens_in.shape
    columns = right_root.shape[3]
    bf16 = jnp.bfloat16
    vmem, anywhere = pl.BlockSpec(memory_space=pltpu.VMEM), pl.BlockSpec(memory_space=pl.ANY)
    done, lefts, rights = pl.pallas_call(
        kernel,
        out_shape=(
            pltpu.VMEM((depth, columns), bf16),
            pltpu.VMEM((8, depth, rows), bf16),
            pltpu.VMEM((8, rows, columns), bf16),
        ),
        in_specs=[anywhere] * 4,
        out_specs=(vmem,) * 3,
        scratch_shapes=[
            pltpu.VMEM((depth, depth), bf16),
            pltpu.VMEM((columns, columns), bf16),
            pltpu.VMEM((rows, depth), bf16),
            pltpu.VMEM((8, rows, columns), bf16),
            pltpu.SemaphoreType.DMA((2,)),
            pltpu.SemaphoreType.DMA,
            pltpu.SemaphoreType.DMA,
            pltpu.SemaphoreType.DMA((9,)),
            pltpu.SemaphoreType.DMA((8,)),
            pltpu.SemaphoreType.DMA((16,)),
            pltpu.SemaphoreType.DMA((16 * PIECES,)),
            pltpu.SemaphoreType.REGULAR,
            pltpu.SemaphoreType.REGULAR,
        ],
        compiler_params=pltpu.CompilerParams(
            collective_id=0, has_side_effects=True, vmem_limit_bytes=40 << 20
        ),
    )(tokens_in, cotangents, left_root[0], right_root[0, 0])
    update = pl.pallas_call(
        ending,
        out_shape=jax.ShapeDtypeStruct((depth, columns), bf16),
        in_specs=[vmem] * 3,
        out_specs=anywhere,
        scratch_shapes=[
            pltpu.VMEM((sum(GROUPS[-1]), columns), bf16),
            pltpu.SemaphoreType.DMA((2,)),
        ],
        compiler_params=pltpu.CompilerParams(vmem_limit_bytes=20 << 20),
    )(done, lefts, rights)
    return update[None]


def solution(mesh):
    placed = (
        P(BOTH, None),
        P(BOTH, None),
        P("expert", None, None),
        P("expert", "replica", None, None),
    )
    return jax.shard_map(
        body, mesh=mesh, in_specs=placed, out_specs=P("expert", None, "replica"), check_vma=False
    )
```

time: 301 us -> 122 us (0.41)
  waiting for transfers between devices: 157 us -> 0 us
  Pallas kernels: 75.1 us -> 122 us
  matrix products: 30.1 us -> 0 us
  local copies, waits for them, and re-layouts: 24.5 us -> 0 us
  between operations: 13.4 us -> 0.01 us
    all_gather x1 -> x0, waiting for transfers between devices: 157 us -> none  [body(): gathered = lax.all_gather(left, 'replica', axis=0, tiled=False)]
    pallas_call x1 -> x2, Pallas kernels: 75.1 us -> 122 us  [the longest x1 119 us: body(): pl.pallas_call(kernel, out_shape=(pltpu.VMEM((depth, columns), bf16), plt...]
    dot_general x3 -> x0, matrix products: 30.1 us -> none  [the longest x1 14.7 us: body(): jnp.einsum('qdt,qtf->df', gathered, right, preferred_element_type=jnp.flo...]
    all_gather x2 -> x0, local copies, waits for them, and re-layouts: 24.4 us -> none  [body(): gathered = lax.all_gather(left, 'replica', axis=0, tiled=False)]
  transfers between devices with their start and end apart: 1 -> 0, of which waited for: 1 -> 0; matrix products, arithmetic and copies ran while one was open for 3% -> 0% of each run, Pallas kernels for 0% -> 0%
where the time goes in v3:
time: 122 us
  Pallas kernels  122 us (100%)
    pallas_call x1, Pallas kernels, body(): pl.pallas_call(kernel, out_shape=(pltpu.VMEM((depth, columns), bf16), plt...  119 us
    pallas_call x1, Pallas kernels, body(): pl.pallas_call(ending, out_shape=jax.ShapeDtypeStruct((depth, columns), b...  3.21 us

profile of v3, /device:TPU:1, one launch (start us, length us, event | category | flops | bytes accessed | tf_op | source)
XLA Modules:
  0.0 121.7 jit_solution(9913826049792042981)
XLA Ops:
  0.0 118.5 %shard_map.46 = (bf16[2048,1024]{1,0:T(8,128)(2,1)S(1)}, bf16[8,2048,256]{2,1,0:T(8,128)(2,1)S(1)}, bf16[8,256,1024]{2,1,0:T(8,128)(2,1)S(1)}) custom-call(bf16[256,2048]{1,0:T(8,128)(2,1)} %tok.1, bf16[256,8192]{1,0:T(8,128)(2,1)} %cot.1, bf16[2048,2048]{1,0:T(8,128)(2,1)} %bitcast.3, bf16[1024,1024]{1,0:T(8,128)(2,1)} %bitcast.4), custom_call_target="tpu_custom_call" | custom-call | tf_op jit(solution)/shard_map/pallas_call | solution.py:322
  118.5 3.2 %shard_map.47 = bf16[2048,1024]{1,0:T(8,128)(2,1)} custom-call(bf16[2048,1024]{1,0:T(8,128)(2,1)S(1)} %get-tuple-element.8.done, bf16[8,2048,256]{2,1,0:T(8,128)(2,1)S(1)} %get-tuple-element.9.lefts, bf16[8,256,1024]{2,1,0:T(8,128)(2,1)S(1)} %get-tuple-element.10.rights), custom_call_target="tpu_custom_call" | custom-call | tf_op jit(solution)/shard_map/pallas_call | solution.py:350

commit v4 on v3

--- a/solution.py
+++ b/solution.py
@@ -10,15 +10,13 @@
 MESH = pl.DeviceIdType.MESH
 SLOTS = 16
 BOTH = ("expert", "replica")
-GROUPS = ((352, 272), (320, 256), (272, 208), (208, 160))
+GROUPS = ((320, 320), (288, 288), (240, 240), (176, 176))
 PIECES = len(GROUPS)
-ROUTED = ()
-OWN = ((0, 1), (2,), (3,), (), (), (), ())
 STEPS = ((2, 0), (2, 1), (1, 0), (1, 1), (3, 0), (3, 1), (0, 0), (0, 1))
-PLAN = ((1, 2, 3, 4), (5, 6, 7), (), (), (), (), ())
+PLAN = ((2, 3, 4), (5, 6), (7,), ())
 LAG = 6
-RIGHTS = (0, 0, 0, 4, 0, 0, 0)
-FINISH = ((), (), (), (0,), (1,), (2,), ())
+RIGHTS = (0, 4, 0, 0)
+SUMS = ((), (0,), (1,), (2,))
 
 
 def pieces():
@@ -31,15 +29,15 @@
     return spans
 
 
-def product(lefts, rights, at, out):
+def product(lefts, rights, chunks, at, out, total=None, into=None):
     @pl.loop(0, rights.shape[2], step=256)
     def _(column):
         to = pl.ds(pl.multiple_of(column, 256), 256)
-        value = None
-        for q in range(8):
+        value = None if total is None else total[at if into is None else into, to]
+        for q in chunks:
             term = jnp.dot(lefts[q, at], rights[q, :, to], preferred_element_type=jnp.float32)
             value = term if value is None else value + term
-        out[:, to] = value.astype(out.dtype)
+        out[at if into is None else into, to] = value.astype(out.dtype)
 
 
 def position():
@@ -65,8 +63,8 @@
 
 
 def kernel(
-    tok, cot, left_hbm, right_hbm, out, lefts, rights,
-    left, right, tokens, routed,
+    tok, cot, left_hbm, right_hbm, out, lefts, rights, total_last,
+    left, right, tokens, routed, total,
     load, tok_send, tok_recv, cot_send, cot_recv, send, recv, plane_sem, all_sem,
 ):
     x, y, z, c = position()
@@ -169,10 +167,8 @@
             there, name = device(beside, y, z, c), (1 - s, dz, part)
         elif to == "above":
             there, name = device(x, y, (z + 1) % 4, c), (s, (dz + 3) % 4, part)
-        elif to == "below":
+        else:
             there, name = device(x, y, (z + 3) % 4, c), (s, (dz + 1) % 4, part)
-        else:
-            there, name = device(x, y, (z + 2) % 4, c), (s, (dz + 2) % 4, part)
         ref = block(s, dz, part)
         kind = (s, dz > 0, part[0] == "a", to == "beside")
         rows = flight.setdefault(kind, [])
@@ -200,15 +196,28 @@
             jnp.bfloat16
         ).reshape(2, 256, columns)
 
-    def multiply(part):
-        at = pl.ds(*parts[part])
-        product(lefts, rights, at, out.at[at])
+    def first_sum(i):
+        for s, dz in ((1, 3), (0, 1)):
+            arrived(s, dz, ("a", i))
+        for dz in (0, 1, 3):
+            arrived(1, dz, ("b", i))
+        first = [chunk(s, dz) for dz in (0, 1, 3) for s in (0, 1)]
+        at = pl.ds(*parts[i])
+        if i + 1 < PIECES:
+            product(lefts, rights, first, at, total)
+        else:
+            product(lefts, rights, first, at, total_last, into=pl.ds(0, at.size))
+
+    def second_sum(i):
+        for s in (0, 1):
+            arrived(s, 2, ("a", i))
+        arrived(1, 2, ("b", i))
+        if i + 1 < PIECES:
+            product(lefts, rights, [chunk(0, 2), chunk(1, 2)], pl.ds(*parts[i]), out, total)
 
     def push_own(part):
         for to in ("beside", "above", "below") if part[0] == "a" else ("above", "below", "beside"):
             push(0, 0, part, to)
-        if part[1] in ROUTED:
-            push(0, 0, part, "over")
 
     waited = []
 
@@ -228,72 +237,51 @@
                 load_right.wait()
             apply_right(turns.pop(0))
 
-    def arrivals(i):
-        part = ("a", i)
-        late = ((0, 3), (1, 1)) if i in ROUTED else ()
-        for s, dz in late + ((1, 3), (0, 1), (0, 2), (1, 2)):
-            arrived(s, dz, part)
-        part = ("b", i)
-        for dz in (0, 1, 3, 2):
-            arrived(1, dz, part)
-
     def push_group(i):
         push_own(("a", i))
         push_own(("b", i))
-
-    ready = [0]
-
-    def prepare(upto):
-        while ready[0] < min(upto, PIECES):
-            apply_left(ready[0])
-            ready[0] += 1
 
     send_near()
     drain(tokens.at[pl.ds(0, 15 * SLOTS)], tok_send)
     send_far(0)
     load_left.wait()
     drain(tokens, tok_recv)
-    prepare(1)
-    for step in range(PIECES + 3):
-        last, older = (i if 0 <= i < PIECES else None for i in (step - 1, step - 2))
-        if older is not None and older not in ROUTED:
-            arrived(0, 3, ("a", older))
-            push(0, 3, ("a", older), "above")
-            arrived(1, 1, ("a", older))
-            push(1, 1, ("a", older), "below")
-        if last is not None:
-            part = ("a", last)
-            arrived(1, 0, part)
-            push(1, 0, part, "above")
-            push(1, 0, part, "below")
-            if last in ROUTED:
-                push(1, 0, part, "over")
-            part = ("b", last)
-            arrived(0, 3, part)
-            arrived(0, 1, part)
-            if last not in ROUTED:
-                if last % 2:
-                    push(0, 1, part, "below")
-                else:
-                    push(0, 3, part, "above")
-            push(0, 1, part, "beside")
-            push(0, 3, part, "beside")
-            if last in ROUTED:
-                arrived(0, 2, part)
-                push(0, 2, part, "beside")
-        for own in OWN[step]:
-            prepare(own + 2)
-            push_group(own)
-        far(PLAN[step])
-        if older is not None and older not in ROUTED:
-            part = ("b", older)
-            arrived(0, 2, part)
-            push(0, 2, part, "beside")
-        some_right(RIGHTS[step])
-        for i in FINISH[step]:
-            arrivals(i)
-            multiply(i)
-    arrivals(PIECES - 1)
+    for i in range(PIECES):
+        apply_left(i)
+        if i:
+            push_group(i - 1)
+    send_far(1)
+    push_group(PIECES - 1)
+    for i in range(PIECES):
+        part = ("a", i)
+        arrived(1, 0, part)
+        push(1, 0, part, "above")
+        push(1, 0, part, "below")
+        far(PLAN[i])
+        part = ("b", i)
+        arrived(0, 3, part)
+        arrived(0, 1, part)
+        if i % 2:
+            push(0, 1, part, "below")
+        else:
+            push(0, 3, part, "above")
+        push(0, 1, part, "beside")
+        push(0, 3, part, "beside")
+    for i in range(PIECES):
+        part = ("a", i)
+        arrived(0, 3, part)
+        push(0, 3, part, "above")
+        arrived(1, 1, part)
+        push(1, 1, part, "below")
+        some_right(RIGHTS[i])
+        part = ("b", i)
+        arrived(0, 2, part)
+        push(0, 2, part, "beside")
+        for j in SUMS[i]:
+            first_sum(j)
+    first_sum(PIECES - 1)
+    for i in range(PIECES):
+        second_sum(i)
 
     for step in range(9):
         if step not in waited:
@@ -303,12 +291,15 @@
         drain(lefts.at[pl.ds(0, times), pl.ds(0, sum(rows) // times)], send.at[i])
 
 
-def ending(done, lefts, rights, out, rest, sems):
+def ending(done, lefts, rights, total, out, rest, sems):
     start, size = pieces()[PIECES - 1]
     whole = pltpu.make_async_copy(done.at[pl.ds(0, start)], out.at[pl.ds(0, start)], sems.at[0])
     whole.start()
-    product(lefts, rights, pl.ds(start, size), rest)
-    last = pltpu.make_async_copy(rest, out.at[pl.ds(start, size)], sems.at[1])
+    at = pl.ds(start, size)
+    z = lax.axis_index("replica") // 2
+    far = ((z + 2) % 4) * 2
+    product(lefts, rights, (far, far + 1), at, rest, total, into=pl.ds(0, size))
+    last = pltpu.make_async_copy(rest, out.at[at], sems.at[1])
     last.start()
     whole.wait()
     last.wait()
@@ -319,20 +310,22 @@
     columns = right_root.shape[3]
     bf16 = jnp.bfloat16
     vmem, anywhere = pl.BlockSpec(memory_space=pltpu.VMEM), pl.BlockSpec(memory_space=pl.ANY)
-    done, lefts, rights = pl.pallas_call(
+    done, lefts, rights, total = pl.pallas_call(
         kernel,
         out_shape=(
             pltpu.VMEM((depth, columns), bf16),
             pltpu.VMEM((8, depth, rows), bf16),
             pltpu.VMEM((8, rows, columns), bf16),
+            pltpu.VMEM((sum(GROUPS[-1]), columns), jnp.float32),
         ),
         in_specs=[anywhere] * 4,
-        out_specs=(vmem,) * 3,
+        out_specs=(vmem,) * 4,
         scratch_shapes=[
             pltpu.VMEM((depth, depth), bf16),
             pltpu.VMEM((columns, columns), bf16),
             pltpu.VMEM((rows, depth), bf16),
             pltpu.VMEM((8, rows, columns), bf16),
+            pltpu.VMEM((depth - sum(GROUPS[-1]), columns), jnp.float32),
             pltpu.SemaphoreType.DMA((2,)),
             pltpu.SemaphoreType.DMA,
             pltpu.SemaphoreType.DMA,
@@ -350,14 +343,14 @@
     update = pl.pallas_call(
         ending,
         out_shape=jax.ShapeDtypeStruct((depth, columns), bf16),
-        in_specs=[vmem] * 3,
+        in_specs=[vmem] * 4,
         out_specs=anywhere,
         scratch_shapes=[
             pltpu.VMEM((sum(GROUPS[-1]), columns), bf16),
             pltpu.SemaphoreType.DMA((2,)),
         ],
         compiler_params=pltpu.CompilerParams(vmem_limit_bytes=20 << 20),
-    )(done, lefts, rights)
+    )(done, lefts, rights, total)
     return update[None]
 
 

time: 122 us -> 119 us (0.975)
  Pallas kernels: 122 us -> 119 us
    pallas_call x1, Pallas kernels: 119 us -> 117 us  [body(): pl.pallas_call(kernel, out_shape=(pltpu.VMEM((depth, columns), bf16), plt...]
where the time goes in v4:
time: 119 us
  Pallas kernels  119 us (100%)
    pallas_call x1, Pallas kernels, body(): pl.pallas_call(kernel, out_shape=(pltpu.VMEM((depth, columns), bf16), plt...  117 us

profile of v4, /device:TPU:1, one launch (start us, length us, event | category | flops | bytes accessed | tf_op | source)
XLA Modules:
  0.0 118.7 jit_solution(7107458266583477701)
XLA Ops:
  0.0 116.7 %shard_map.46 = (bf16[2048,1024]{1,0:T(8,128)(2,1)S(1)}, bf16[8,2048,256]{2,1,0:T(8,128)(2,1)S(1)}, bf16[8,256,1024]{2,1,0:T(8,128)(2,1)S(1)}, f32[352,1024]{1,0:T(8,128)S(1)}) custom-call(bf16[256,2048]{1,0:T(8,128)(2,1)} %tok.1, bf16[256,8192]{1,0:T(8,128)(2,1)} %cot.1, bf16[2048,2048]{1,0:T(8,128)(2,1)} %bitcast.3, bf16[1024,1024]{1,0:T(8,128)(2,1)} %bitcast.4), custom_call_target="tpu_custom_call" | custom-call | tf_op jit(solution)/shard_map/pallas_call | solution.py:313
  116.7 2.0 %shard_map.47 = bf16[2048,1024]{1,0:T(8,128)(2,1)} custom-call(bf16[2048,1024]{1,0:T(8,128)(2,1)S(1)} %get-tuple-element.9.done, bf16[8,2048,256]{2,1,0:T(8,128)(2,1)S(1)} %get-tuple-element.10.lefts, bf16[8,256,1024]{2,1,0:T(8,128)(2,1)S(1)} %get-tuple-element.11.rights, f32[352,1024]{1,0:T(8,128)S(1)} %get-tuple-element.12.total), custom_call_target="tpu_custom_call" | custom-call | tf_op jit(solution)/shard_map/pallas_call | solution.py:343

commit v5 on v4

--- a/solution.py
+++ b/solution.py
@@ -12,10 +12,11 @@
 BOTH = ("expert", "replica")
 GROUPS = ((320, 320), (288, 288), (240, 240), (176, 176))
 PIECES = len(GROUPS)
-STEPS = ((2, 0), (2, 1), (1, 0), (1, 1), (3, 0), (3, 1), (0, 0), (0, 1))
+STEPS = ((0, 0, 0), (0, 0, 1), (0, 1, 0), (0, 1, 1), (1, 0, 0), (1, 0, 1), (1, 1, 0), (1, 1, 1))
 PLAN = ((2, 3, 4), (5, 6), (7,), ())
 LAG = 6
-RIGHTS = (0, 4, 0, 0)
+RIGHTS = (0, 0, 0, 2, 0, 2, 0, 0)
+ZERO = ((), (), (), (0, 1, 2, 3), (), (), (), ())
 SUMS = ((), (0,), (1,), (2,))
 
 
@@ -139,11 +140,11 @@
         lax.fori_loop(1, 16, one, 0)
 
     def send_far(step):
-        lift, core = STEPS[step]
+        odd, turn, core = STEPS[step]
 
         def one(k, _):
             a, b = k % 4, k // 4
-            send_one(step, a, (a + b) % 4, (a + lift) % 4, core)
+            send_one(step, a, (a + b) % 4, odd + 2 * ((a + turn) % 2), core)
             return 0
 
         lax.fori_loop(1, 13, one, 0)
@@ -196,17 +197,23 @@
             jnp.bfloat16
         ).reshape(2, 256, columns)
 
+    def add(i, chunks, begin=False):
+        at = pl.ds(*parts[i])
+        if i + 1 < PIECES:
+            product(lefts, rights, chunks, at, total, None if begin else total)
+        else:
+            product(lefts, rights, chunks, at, total_last, None if begin else total_last, pl.ds(0, at.size))
+
+    def zero_sum(i):
+        arrived(1, 0, ("b", i))
+        add(i, [chunk(0, 0), chunk(1, 0)], True)
+
     def first_sum(i):
         for s, dz in ((1, 3), (0, 1)):
             arrived(s, dz, ("a", i))
-        for dz in (0, 1, 3):
+        for dz in (1, 3):
             arrived(1, dz, ("b", i))
-        first = [chunk(s, dz) for dz in (0, 1, 3) for s in (0, 1)]
-        at = pl.ds(*parts[i])
-        if i + 1 < PIECES:
-            product(lefts, rights, first, at, total)
-        else:
-            product(lefts, rights, first, at, total_last, into=pl.ds(0, at.size))
+        add(i, [chunk(s, dz) for dz in (1, 3) for s in (0, 1)])
 
     def second_sum(i):
         for s in (0, 1):
@@ -229,7 +236,7 @@
                 waited.append(old)
             send_far(step)
 
-    turns = [0, 1, 3, 2]
+    turns = [0, 2, 1, 3]
 
     def some_right(count):
         for _ in range(count):
@@ -267,16 +274,21 @@
             push(0, 3, part, "above")
         push(0, 1, part, "beside")
         push(0, 3, part, "beside")
+        some_right(RIGHTS[i])
+        for j in ZERO[i]:
+            zero_sum(j)
     for i in range(PIECES):
         part = ("a", i)
         arrived(0, 3, part)
         push(0, 3, part, "above")
         arrived(1, 1, part)
         push(1, 1, part, "below")
-        some_right(RIGHTS[i])
+        some_right(RIGHTS[PIECES + i])
         part = ("b", i)
         arrived(0, 2, part)
         push(0, 2, part, "beside")
+        for j in ZERO[PIECES + i]:
+            zero_sum(j)
         for j in SUMS[i]:
             first_sum(j)
     first_sum(PIECES - 1)

time: 119 us -> 119 us (level)
  no operation moved by 1% of the time
where the time goes in v5:
time: 119 us
  Pallas kernels  119 us (100%)
    pallas_call x1, Pallas kernels, body(): pl.pallas_call(kernel, out_shape=(pltpu.VMEM((depth, columns), bf16), plt...  117 us

profile of v5, /device:TPU:1, one launch (start us, length us, event | category | flops | bytes accessed | tf_op | source)
XLA Modules:
  0.0 118.9 jit_solution(2408684443200788064)
XLA Ops:
  0.0 116.9 %shard_map.46 = (bf16[2048,1024]{1,0:T(8,128)(2,1)S(1)}, bf16[8,2048,256]{2,1,0:T(8,128)(2,1)S(1)}, bf16[8,256,1024]{2,1,0:T(8,128)(2,1)S(1)}, f32[352,1024]{1,0:T(8,128)S(1)}) custom-call(bf16[256,2048]{1,0:T(8,128)(2,1)} %tok.1, bf16[256,8192]{1,0:T(8,128)(2,1)} %cot.1, bf16[2048,2048]{1,0:T(8,128)(2,1)} %bitcast.3, bf16[1024,1024]{1,0:T(8,128)(2,1)} %bitcast.4), custom_call_target="tpu_custom_call" | custom-call | tf_op jit(solution)/shard_map/pallas_call | solution.py:325
  116.9 2.0 %shard_map.47 = bf16[2048,1024]{1,0:T(8,128)(2,1)} custom-call(bf16[2048,1024]{1,0:T(8,128)(2,1)S(1)} %get-tuple-element.9.done, bf16[8,2048,256]{2,1,0:T(8,128)(2,1)S(1)} %get-tuple-element.10.lefts, bf16[8,256,1024]{2,1,0:T(8,128)(2,1)S(1)} %get-tuple-element.11.rights, f32[352,1024]{1,0:T(8,128)S(1)} %get-tuple-element.12.total), custom_call_target="tpu_custom_call" | custom-call | tf_op jit(solution)/shard_map/pallas_call | solution.py:355
